TPU v7x, 256 devices: a whole 4x4x8 slice. The times are simulated.
256 devices in a mesh: task: 32 (over x, z_hi, core), mp: 8 (over y, z_lo).
Axes of the slice: x: 4, y: 4, z: 8 (z_hi: 4, z_lo: 2; z = z_hi * 2 + z_lo), core: 2. Of those that a mesh axis runs over, the one named last changes fastest.
Arguments:
- hidden_in: bfloat16 [32768, 1024], P(('task', 'mp')), parts along dimension 0, may hold values from -16 to 16
- ff_gain: float32 [1024], replicated, may hold values from 0.5 to 1.5
- w_gate: bfloat16 [1024, 3072], P(None, 'mp'), may hold values from -0.1875 to 0.1875
- w_up: bfloat16 [1024, 3072], P(None, 'mp'), may hold values from -0.1875 to 0.1875
- w_out: bfloat16 [3072, 1024], P('mp'), may hold values from -0.109375 to 0.109375
- ff_rescale: float32 [98304], P(('task', 'mp')), parts along dimension 0, may hold values from 0.5 to 2
- final_gain: float32 [1024], replicated, may hold values from 0.5 to 1.5
- w_head: bfloat16 [1024, 16384], P(None, 'mp'), may hold values from -8 to 8
- targets: int32 [32768], P('task'), parts along dimension 0, may hold values from 0 to 16383
- lengths: int32 [128, 4], P('task'), parts along dimension 0, may hold values from 1 to 64, as said below
- labels: int32 [128], P('task'), parts along dimension 0, may hold values from 0 to 3
Outputs:
- scale_grad: float32 [98304], P(('task', 'mp')), parts along dimension 0
- loss_value: float32 [32], P('task'), parts along dimension 0
There are 32 independent parts, one for each index of `task`. A program takes and returns all parts, laid end to end along the dimension named above; an argument that names none is the same for every part. Nothing has to cross between parts.
Inputs may be any that keep to these rules, and one draw needn't show every extreme that they name: `lengths`: every answer choice has at least one target token.
All inputs are finite; a program needn't handle non-finite values.
Results may differ from a plain program's by a relative error of at most 0.0067.
Values may be sent and summed in bfloat16 or wider, within the bound.
A program may use at most 64 MiB of HBM per device.

v0:
```python
import jax
import jax.numpy as jnp
from jax import lax
from jax.sharding import PartitionSpec as P

epsilon = 1e-06


def sent_to_all(x, axis):
    copies = jnp.broadcast_to(x, (lax.axis_size(axis), *x.shape))
    return lax.all_to_all(copies, axis, split_axis=0, concat_axis=0, tiled=True)


def joined_along(pieces, dim):
    dims = list(pieces.shape[1:])
    dims[dim] *= pieces.shape[0]
    return jnp.moveaxis(pieces, 0, dim).reshape(dims)


def gathered_copies(x, axis, dim):
    pieces = sent_to_all(x, axis)
    return joined_along(pieces, dim)


def cut_along(x, dim, count):
    dims = x.shape
    pieces = x.reshape(*dims[:dim], count, dims[dim] // count, *dims[dim + 1 :])
    return jnp.moveaxis(pieces, dim, 0)


def summed_on_arrival(x, axis, dim):
    count = lax.axis_size(axis)
    pieces = lax.all_to_all(cut_along(x, dim, count), axis, 0, 0, tiled=True)
    return jnp.sum(pieces, axis=0)


def gathered_once(x, axis):
    leaves = jax.tree.leaves(x)
    turns = sorted(range(len(leaves)), key=lambda k: -leaves[k].size)
    width = (1, *leaves[turns[0]].shape)[-1]
    lines = [
        jnp.pad(leaves[k].reshape(-1), (0, -leaves[k].size % width)).reshape(-1, width)
        for k in turns
    ]
    both, at, found = (lax.all_gather(jnp.concatenate(lines), axis), 0, {})
    for k, line in zip(turns, lines):
        slab = both[:, at : at + len(line)].reshape(len(both), -1)
        found[k] = slab[:, : leaves[k].size].reshape(-1, *leaves[k].shape)
        at += len(line)
    numbers = iter(range(len(leaves)))
    return jax.tree.map(lambda _: found[next(numbers)], x)


def combined_all(x, axis, combine):
    everything = gathered_once(x, axis)
    initial = jax.tree.map(lambda part: part[0], everything)

    def lap(k, so_far):
        return combine(so_far, jax.tree.map(lambda part: part[k], everything))

    return lax.fori_loop(1, lax.axis_size(axis), lap, initial)


def rms_scale(values, gain):
    inverse = lax.rsqrt(jnp.mean(values * values, axis=-1, keepdims=True) + epsilon)
    return (values * inverse * gain, inverse)


def norm_back(values, inverse, gain, upstream):
    scaled = upstream * gain
    return inverse * scaled - values * inverse**3 * jnp.mean(
        scaled * values, axis=-1, keepdims=True
    )


def task_loss(log_probs, lengths, labels):
    examples, choices = lengths.shape
    length = log_probs.shape[0] // (examples * choices)
    number_type = log_probs.dtype
    shaped = log_probs.reshape(examples, choices, length)
    position = jnp.arange(length, dtype=jnp.int32)
    valid = (position[None, None, :] < lengths[:, :, None]).astype(number_type)
    counts = lengths.astype(number_type)
    summed = jnp.sum(shaped * valid, axis=-1)
    average = summed / counts
    correct = (jnp.arange(choices, dtype=jnp.int32)[None, :] == labels[:, None]).astype(number_type)
    wrong = 1.0 - correct
    likely = -jnp.sum(summed * correct) / jnp.sum(counts * correct)
    safe = jnp.where(valid > 0, shaped, -1.0)
    unlikely = -jnp.sum(jnp.log1p(-jnp.exp(safe)) * valid * wrong[:, :, None]) / jnp.sum(
        counts * wrong
    )
    normed = -jnp.mean(jnp.sum(jax.nn.log_softmax(average, axis=-1) * correct, axis=-1))
    return likely + unlikely + normed


def pair_merge(first, second):
    first_max, first_sum, first_target = first
    second_max, second_sum, second_target = second
    joint_max = jnp.maximum(first_max, second_max)
    joint_sum = first_sum * jnp.exp(first_max - joint_max) + second_sum * jnp.exp(
        second_max - joint_max
    )
    return (joint_max, joint_sum, first_target + second_target)


def per_device(
    hidden_in,
    ff_gain,
    w_gate,
    w_up,
    w_out,
    ff_rescale,
    final_gain,
    w_head,
    targets,
    lengths,
    labels,
):
    place = lax.axis_index("mp")
    contract = (((1,), (1,)), ((), ()))
    inputs = hidden_in.astype(jnp.float32)
    normed_in = rms_scale(inputs, ff_gain)[0].astype(jnp.bfloat16)
    width = w_gate.shape[1]
    shard_rows = gathered_copies(normed_in, "mp", 0)
    gate_part = jnp.dot(shard_rows, w_gate, preferred_element_type=jnp.float32)
    up_part = jnp.dot(shard_rows, w_up, preferred_element_type=jnp.float32)
    projected = jnp.concatenate([gate_part, up_part], axis=1)
    activated = jax.nn.gelu(projected[:, :width], approximate=True) * projected[:, width:]
    hidden = (activated * ff_rescale).astype(jnp.bfloat16)
    residual = (
        summed_on_arrival(jnp.dot(hidden, w_out, preferred_element_type=jnp.float32), "mp", 0)
        + inputs
    )
    normed_out, inverse = rms_scale(residual, final_gain)
    logits = jnp.dot(
        gathered_copies(normed_out.astype(jnp.bfloat16), "mp", 0),
        w_head,
        preferred_element_type=jnp.float32,
    )
    vocab_own = logits.shape[1]
    columns = jnp.arange(vocab_own, dtype=jnp.int32)[None, :]
    is_target = columns == (targets - place * vocab_own)[:, None]
    target_part = jnp.sum(jnp.where(is_target, logits, 0.0), axis=1)
    local_max = jnp.max(logits, axis=1)
    local_sum = jnp.sum(jnp.exp(logits - local_max[:, None]), axis=1)
    row_max, row_sum, target_logit = combined_all(
        (local_max, local_sum, target_part), "mp", pair_merge
    )
    log_norm = row_max + jnp.log(row_sum)
    log_probs = target_logit - log_norm
    loss_value, pullback = jax.vjp(lambda values: task_loss(values, lengths, labels), log_probs)
    (token_weight,) = pullback(jnp.ones_like(loss_value))
    softmax_rows = jnp.exp(logits - log_norm[:, None])
    logit_grad = (token_weight[:, None] * (is_target.astype(jnp.float32) - softmax_rows)).astype(
        jnp.bfloat16
    )
    normed_grad = summed_on_arrival(
        lax.dot_general(logit_grad, w_head, contract, preferred_element_type=jnp.float32), "mp", 0
    )
    resid_grad = norm_back(residual, inverse, final_gain, normed_grad).astype(jnp.bfloat16)
    hidden_grad = lax.dot_general(
        lax.all_gather(resid_grad, "mp", axis=0, tiled=True),
        w_out,
        contract,
        preferred_element_type=jnp.float32,
    )
    scale_grad = jnp.sum(hidden_grad * activated, axis=0)
    return (scale_grad, loss_value.reshape(1))


def solution(mesh):
    return jax.shard_map(
        per_device,
        mesh=mesh,
        in_specs=(
            P(("task", "mp"), None),
            P(),
            P(None, "mp"),
            P(None, "mp"),
            P("mp", None),
            P(("task", "mp")),
            P(),
            P(None, "mp"),
            P("task"),
            P("task", None),
            P("task"),
        ),
        out_specs=(P(("task", "mp")), P("task")),
        check_vma=False,
    )
```

profile of v0, /device:TPU:4, one launch (start us, length us, event | category | flops | bytes accessed | tf_op | source)
XLA Modules:
  0.0 303.5 jit_solution(508517285441279573)
XLA Ops:
  7.2 0.0 copy-start
  7.2 1.2 fusion.14
  8.3 1.1 fusion.16
  9.4 0.3 broadcast_in_dim.32
  9.7 0.0 copy-start.8
  9.7 33.0 %all_to_all.20 = bf16[8,128,1024]{2,1,0:T(8,128)(2,1)S(1)} all-to-all(bf16[8,128,1024]{2,1,0:T(8,128)(2,1)S(1)} %broadcast_in_dim.32), channel_id=1, replica_groups=mesh['task'=32,'mp'=8] {'mp'}, dimensions={0} | all-to-all | bytes 4194304 | tf_op jit(solution)/shard_map/all_to_all | solution.py:11
  42.7 0.0 copy-done.8
  42.7 0.0 copy-start.9
  42.7 1.3 fusion.24
  44.0 0.0 copy-done.9
  44.0 0.0 copy-start.5
  44.0 1.4 fusion.11
  45.4 0.0 copy-done
  45.4 0.0 copy-done.5
  45.5 1.2 fusion.12
  46.7 51.8 %all_to_all.21 = f32[8,128,1024]{2,1,0:T(8,128)} all-to-all(f32[8,128,1024]{2,1,0:T(8,128)S(1)} %bitcast.39), channel_id=1, replica_groups=mesh['task'=32,'mp'=8] {'mp'}, dimensions={0} | all-to-all | bytes 8388608 | tf_op jit(solution)/shard_map/all_to_all | solution.py:33
  98.5 0.0 copy-start.1
  98.5 0.0 copy-start.4
  98.5 2.6 reduce_sum.156
  101.2 0.0 copy-done.1
  101.2 0.2 multiply_reduce_fusion.2
  101.3 0.0 copy-done.4
  101.3 0.1 multiply_convert_fusion.4
  101.5 1.6 broadcast_in_dim.56
  103.0 0.0 copy-start.3
  103.0 0.0 copy-start.6
  103.0 0.0 copy-start.7
  103.0 4.5 %all-to-all-start.2 = ((bf16[8,128,1024]{2,1,0:T(8,128)(2,1)}), bf16[8,128,1024]{2,1,0:T(8,128)(2,1)}, u32[]{:S(2)}, u32[]{:S(2)}) async-start(bf16[8,128,1024]{2,1,0:T(8,128)(2,1)} %broadcast_in_dim.56), calls=%async_computation.2 | async-start | bytes 4194304 | tf_op jit(solution)/shard_map/all_to_all | solution.py:11
  107.5 0.0 all-gather.4.cloned.1.call-start
  107.6 0.0 copy-done.3
  107.6 0.1 iota_compare_fusion.1
  107.7 0.1 lt.41
  107.7 0.0 copy-done.6
  107.7 0.1 convert_subtract_fusion
  107.8 0.1 mul.237
  107.9 0.1 mul.238
  108.0 0.0 copy-done.7
  108.0 24.8 %all-to-all-done.2 = bf16[8,128,1024]{2,1,0:T(8,128)(2,1)} async-done(((bf16[8,128,1024]{2,1,0:T(8,128)(2,1)}), bf16[8,128,1024]{2,1,0:T(8,128)(2,1)}, u32[]{:S(2)}, u32[]{:S(2)}) %all-to-all-start.2) | async-done | bytes 2097184 | tf_op jit(solution)/shard_map/all_to_all | solution.py:11
  132.8 7.1 %fusion.23 = (f32[1024]{0:T(1024)S(1)}, f32[1024,2048]{1,0:T(8,128)S(1)}) fusion(bf16[1024,1024]{1,0:T(8,128)(2,1)} %bitcast.5, bf16[1024,2048]{1,0:T(8,128)(2,1)} %param.20), kind=kOutput, calls=%fused_computation.68 | convolution fusion | flops 4297063424 | bytes 14684160 | tf_op jit(solution)/shard_map/dot_general | solution.py:136
  139.8 0.0 copy-start.2
  139.8 2.6 exponential_reduce_fusion
  142.4 0.7 copy-done.2
  143.1 28.4 %all-gather.1 = f32[8,3,1024]{2,1,0:T(4,128)S(1)} all-gather(f32[1,3,1024]{2,1,0:T(4,128)S(1)} %maximum_bitcast_fusion), channel_id=2, replica_groups=mesh['task'=32,'mp'=8] {'mp'}, dimensions={0}, use_global_device_ids=true | all-gather | bytes 110592 | tf_op jit(solution)/shard_map/all_gather | solution.py:45
  171.5 0.1 fusion.21
  171.6 0.6 while.19
  172.2 0.6 multiply_reduce_fusion.3
  172.9 0.1 reshape.158
  172.9 0.2 select_reduce_fusion.1
  173.1 0.1 fusion.20
  173.2 0.2 exponential_reduce_fusion.1
  173.4 0.7 select_reduce_fusion.3
  175.5 0.1 fusion.19
  175.5 0.1 mul.212
  175.6 0.1 mul.213
  175.7 0.1 broadcast_in_dim.62
  175.8 0.1 broadcast_in_dim.63
  175.9 8.8 %fusion = f32[1024,1024]{1,0:T(8,128)S(1)} fusion(bf16[1024,2048]{1,0:T(8,128)(2,1)} %param.20, f32[1024,2048]{1,0:T(8,128)} %copy-done.2, f32[1024]{0:T(1024)S(1)} %get-tuple-element.210, f32[1024]{0:T(1024)S(1)} %select_add_fusion, s32[1024]{0:T(1024)S(1)} %broadcast_subtract_fusion), kind=kOutput, calls=%fused_computation.8 | convolution fusion | flops 4307550208 | bytes 16789504 | tf_op jit(solution)/shard_map/dot_general | solution.py:159
  184.7 45.9 %all_to_all.22 = f32[8,128,1024]{2,1,0:T(8,128)} all-to-all(f32[8,128,1024]{2,1,0:T(8,128)S(1)} %bitcast.40), channel_id=1, replica_groups=mesh['task'=32,'mp'=8] {'mp'}, dimensions={0} | all-to-all | bytes 8388608 | tf_op jit(solution)/shard_map/all_to_all | solution.py:33
  230.6 3.4 %reduce_sum.165 = f32[128,1024]{1,0:T(8,128)} reduce(f32[8,128,1024]{2,1,0:T(8,128)} %all_to_all.22, f32[]{:T(128)} %constant.79.clone.1), dimensions={0}, to_apply=%region_14.15 | reduce | flops 917504 | bytes 4718596 | tf_op jit(solution)/shard_map/reduce_sum | solution.py:34
  234.0 1.2 multiply_reduce_fusion.1
  235.2 2.0 subtract_convert_fusion
  237.1 0.0 all-gather.4.cloned.1.call-update
  240.3 51.8 %all-gather.4.cloned.1.call-done = bf16[1024,1024]{1,0:T(8,128)(2,1)} async-done(((bf16[128,1024]{1,0:T(8,128)(2,1)}), bf16[1024,1024]{1,0:T(8,128)(2,1)}) %all-gather.4.cloned.1.call-update) | async-done | bytes 2097168 | tf_op jit(solution)/shard_map/all_gather | solution.py:163
  292.1 3.5 %multiply_reduce_fusion = f32[384]{0:T(512)} fusion(f32[1024,384]{1,0:T(8,128)S(1)} %fusion.11, bf16[1024,1024]{1,0:T(8,128)(2,1)} %all-gather.4.cloned.1.call-done, bf16[384,1024]{1,0:T(8,128)(2,1)S(1)} %copy-done), kind=kOutput, calls=%fused_computation.21 | convolution fusion | flops 806092416 | bytes 4457984 | tf_op jit(solution)/shard_map/dot_general | solution.py:162
  (39 shorter events, 0.4 us)
Async XLA Ops:
  7.2 38.3 %copy-start = (bf16[384,1024]{1,0:T(8,128)(2,1)S(1)}, bf16[384,1024]{1,0:T(8,128)(2,1)}, u32[]{:S(2)}) copy-start(bf16[384,1024]{1,0:T(8,128)(2,1)} %param.17) | copy-start | bytes 2359300
  9.7 33.0 %copy-start.8 = (bf16[1024,384]{1,0:T(8,128)(2,1)S(1)}, bf16[1024,384]{1,0:T(8,128)(2,1)}, u32[]{:S(2)}) copy-start(bf16[1024,384]{1,0:T(8,128)(2,1)} %param.15) | copy-start | bytes 2359300
  42.7 1.3 copy-start.9
  44.0 1.5 copy-start.5
  98.5 2.7 copy-start.1
  98.5 2.8 copy-start.4
  103.0 4.5 %copy-start.3 = (s32[4,4]{1,0:T(4,128)S(1)}, s32[4,4]{1,0:T(4,128)}, u32[]{:S(2)}) copy-start(s32[4,4]{1,0:T(4,128)} %param.22) | copy-start | bytes 196
  103.0 4.7 %copy-start.6 = (s32[4]{0:T(128)S(1)}, s32[4]{0:T(128)}, u32[]{:S(2)}) copy-start(s32[4]{0:T(128)} %param.23) | copy-start | bytes 52
  103.0 4.9 %copy-start.7 = (s32[1024]{0:T(1024)S(1)}, s32[1024]{0:T(1024)}, u32[]{:S(2)}) copy-start(s32[1024]{0:T(1024)} %param.21) | copy-start | bytes 12292
  103.0 29.7 %all-to-all-start.2 = ((bf16[8,128,1024]{2,1,0:T(8,128)(2,1)}), bf16[8,128,1024]{2,1,0:T(8,128)(2,1)}, u32[]{:S(2)}, u32[]{:S(2)}) async-start(bf16[8,128,1024]{2,1,0:T(8,128)(2,1)} %broadcast_in_dim.56), calls=%async_computation.2 | async-start | bytes 4194304 | tf_op jit(solution)/shard_map/all_to_all | solution.py:11
  107.5 184.6 %all-gather.4.cloned.1.call-start = ((), (), s32[]{:S(2)}) async-start(), calls=%async_computation.4 | async-start | bytes 2359296 | tf_op jit(solution)/shard_map/all_gather | solution.py:163
  139.8 3.2 %copy-start.2 = (f32[1024,2048]{1,0:T(8,128)}, f32[1024,2048]{1,0:T(8,128)S(1)}, u32[]{:S(2)}) copy-start(f32[1024,2048]{1,0:T(8,128)S(1)} %get-tuple-element.226) | copy-start | bytes 25165828
Sparse Core Ops, SparseCore 0:
  237.3 54.7 all-gather.3
where the time goes:
time: 304 us
  blocking collectives  159 us (52%)
  waiting for transfers between devices  76.6 us (25%)
  matrix products  23.3 us (8%)
  between operations  19.8 us (7%)
  other arithmetic  16.5 us (5%)
  starting transfers between devices  4.51 us (1%)
  local copies, waits for them, and re-layouts  3.4 us (1%)
    all_to_all x2, blocking collectives, summed_on_arrival(): pieces = lax.all_to_all(cut_along(x, dim, count), axis, 0, 0, tiled=True)  97.7 us
    all_gather x1, waiting for transfers between devices, per_device(): lax.all_gather(resid_grad, 'mp', axis=0, tiled=True)  51.8 us
    all_to_all x1, blocking collectives, sent_to_all(): return lax.all_to_all(copies, axis, split_axis=0, concat_axis=0, tiled=True)  33 us
    all_gather x1, blocking collectives, gathered_once(): both, at, found = (lax.all_gather(jnp.concatenate(lines), axis), 0, {})  28.4 us
    all_to_all x1, waiting for transfers between devices, sent_to_all(): return lax.all_to_all(copies, axis, split_axis=0, concat_axis=0, tiled=True)  24.8 us
    dot_general x1, matrix products, per_device(): lax.dot_general(logit_grad, w_head, contract, preferred_element_type=jnp....  8.79 us
    dot_general x1, matrix products, per_device(): jnp.dot(gathered_copies(normed_out.astype(jnp.bfloat16), 'mp', 0), w_head...  7.07 us
  transfers between devices with their start and end apart: 2, of which 2 were waited for; matrix products, arithmetic and copies ran while one was open for 0% of the time, Pallas kernels for 0%

commit v1 on v0

v1 whole, which is shorter than its diff:
```python
import functools
import math

import jax
import jax.numpy as jnp
from jax import lax
from jax.experimental import pallas as pl
from jax.experimental.pallas import tpu as pltpu
from jax.sharding import PartitionSpec as P

f32 = jnp.float32
bf16 = jnp.bfloat16
epsilon = 1e-06
ROOT = math.sqrt(2.0 / math.pi)
TILE = 512
STEPS = 256.0
TOP = 32700.0
WIDE = 1024 + 128

A, B = (0, 2), (2, 2)
AP, AM, BP, BM = (0, 1), (1, 1), (2, 1), (3, 1)


def coded(total):
    top = jnp.max(jnp.abs(total), axis=-1, keepdims=True)
    top = jnp.broadcast_to(jnp.maximum(top, 1e-30), (*total.shape[:-1], 128))
    power = jnp.ceil(jnp.log(top) * (STEPS / math.log(2.0)))
    factor = TOP * jnp.exp(power * (-math.log(2.0) / STEPS))
    value = jnp.round(total * jnp.concatenate([factor] * 8, axis=-1))
    both = jnp.concatenate([value, power], axis=-1)
    return both.astype(jnp.int32).astype(jnp.int16)


def decoded(code):
    both = code.astype(jnp.int32).astype(f32)
    factor = jnp.exp(both[..., 1024:] * (math.log(2.0) / STEPS)) * (1.0 / TOP)
    return both[..., :1024] * jnp.concatenate([factor] * 8, axis=-1)


class Links:
    def __init__(self, place, sends, recvs, log):
        y, z = place // 2, place % 2
        self.y, self.z = y, z
        self.yp, self.ym, self.yo = (y + 1) % 4, (y + 3) % 4, (y + 2) % 4
        self.oz = 1 - z
        self.to = {"z": y * 2 + (1 - z), "p": self.yp * 2 + z, "m": self.ym * 2 + z}
        self.sends, self.recvs, self.log = sends, recvs, log

    def copy(self, k, src, dst, way):
        return pltpu.make_async_remote_copy(
            src_ref=src,
            dst_ref=dst,
            send_sem=self.sends.at[k],
            recv_sem=self.recvs.at[k],
            device_id={"mp": self.to[way]},
            device_id_type=pl.DeviceIdType.MESH,
        )

    def send(self, k, src, dst, way):
        c = self.copy(k, src, dst, way)
        c.start()
        self.log.append(c)

    def got(self, k, dst):
        self.copy(k, dst, dst, "z").wait_recv()


class Gather(Links):
    def __init__(self, place, at, sends, recvs, log):
        super().__init__(place, sends, recvs, log)
        self.at = at

    def put(self, k, y, z, part, way):
        ref = self.at(y, z, part)
        self.send(k, ref, ref, way)

    def have(self, k, y, z, part):
        self.got(k, self.at(y, z, part))

    def s0(self):
        y, z = self.y, self.z
        self.put(0, y, z, A, "z")
        self.put(2, y, z, B, "p")
        self.put(3, y, z, B, "m")
        self.put(1, y, z, B, "z")
        self.put(4, y, z, A, "p")
        self.put(5, y, z, A, "m")

    def r1(self):
        self.have(2, self.ym, self.z, B)
        self.put(6, self.ym, self.z, BP, "p")
        self.put(15, self.ym, self.z, B, "z")
        self.have(3, self.yp, self.z, B)
        self.put(7, self.yp, self.z, BM, "m")
        self.put(14, self.yp, self.z, B, "z")

    def r2(self):
        self.have(0, self.y, self.oz, A)
        self.put(8, self.y, self.oz, A, "p")
        self.put(9, self.y, self.oz, A, "m")

    def r3(self):
        self.have(4, self.ym, self.z, A)
        self.put(10, self.ym, self.z, AP, "p")
        self.have(5, self.yp, self.z, A)
        self.put(11, self.yp, self.z, AM, "m")

    def r4(self):
        self.have(6, self.yo, self.z, BP)
        self.put(16, self.yo, self.z, BP, "z")
        self.have(7, self.yo, self.z, BM)
        self.put(17, self.yo, self.z, BM, "z")

    def r5(self):
        self.have(8, self.ym, self.oz, A)
        self.put(12, self.ym, self.oz, AP, "p")
        self.have(9, self.yp, self.oz, A)
        self.put(13, self.yp, self.oz, AM, "m")

    def own(self):
        self.have(1, self.y, self.oz, B)

    def plus(self):
        self.have(14, self.yp, self.oz, B)

    def minus(self):
        self.have(15, self.ym, self.oz, B)

    def far(self):
        self.have(10, self.yo, self.z, AP)
        self.have(11, self.yo, self.z, AM)
        self.have(12, self.yo, self.oz, AP)
        self.have(13, self.yo, self.oz, AM)
        self.have(16, self.yo, self.oz, BP)
        self.have(17, self.yo, self.oz, BM)


class Sum(Links):
    def __init__(self, place, g, part, out, halves, quarters, sends, recvs, log):
        super().__init__(place, sends, recvs, log)
        self.g, self.part, self.out, self.halves, self.quarters = g, part, out, halves, quarters

    def at(self, ref, y, z, part):
        return ref.at[self.g * 4 + y, z, pl.ds(*part)]

    def h(self, k):
        return self.halves.at[self.g, k]

    def q(self, k):
        return self.quarters.at[self.g, k]

    def s0_far(self):
        yo = self.yo
        for z in range(2):
            self.send(4 + 9 * z, self.at(self.out, yo, z, AP), self.q(0 + z), "p")
            self.send(5 + 9 * z, self.at(self.out, yo, z, AM), self.q(2 + z), "m")
        self.send(0, self.at(self.out, yo, self.oz, B), self.h(0), "z")

    def s0_plus(self):
        self.send(1, self.at(self.out, self.yp, self.oz, B), self.h(1), "z")

    def s0_minus(self):
        self.send(2, self.at(self.out, self.ym, self.oz, B), self.h(2), "z")

    def s0_own(self):
        self.send(3, self.at(self.out, self.y, self.oz, B), self.h(3), "z")

    def add(self, y, z, part, *refs):
        total = self.at(self.part, y, z, part)[...]
        for ref in refs:
            total = total + decoded(ref[...])
        self.at(self.out, y, z, part)[...] = coded(total)

    def s1(self):
        self.got(0, self.h(0))
        self.add(self.yo, self.z, B, self.h(0))
        self.send(8, self.at(self.out, self.yo, self.z, BP), self.q(4), "p")
        self.send(9, self.at(self.out, self.yo, self.z, BM), self.q(5), "m")
        for z in range(2):
            self.got(4 + 9 * z, self.q(0 + z))
            self.add(self.yp, z, AP, self.q(0 + z))
            self.send(6 + 9 * z, self.at(self.out, self.yp, z, A), self.h(4 + z), "p")
            self.got(5 + 9 * z, self.q(2 + z))
            self.add(self.ym, z, AM, self.q(2 + z))
            self.send(7 + 9 * z, self.at(self.out, self.ym, z, A), self.h(6 + z), "m")

    def s2(self):
        self.got(1, self.h(1))
        self.got(8, self.q(4))
        h = self.h(1)
        self.add(self.yp, self.z, BP, h.at[pl.ds(0, 1)], self.q(4))
        self.add(self.yp, self.z, BM, h.at[pl.ds(1, 1)])
        self.send(10, self.at(self.out, self.yp, self.z, B), self.h(8), "p")
        self.got(2, self.h(2))
        self.got(9, self.q(5))
        h = self.h(2)
        self.add(self.ym, self.z, BP, h.at[pl.ds(0, 1)])
        self.add(self.ym, self.z, BM, h.at[pl.ds(1, 1)], self.q(5))
        self.send(11, self.at(self.out, self.ym, self.z, B), self.h(9), "m")

    def s3(self):
        for z in range(2):
            self.got(6 + 9 * z, self.h(4 + z))
            self.got(7 + 9 * z, self.h(6 + z))
        self.add(self.y, self.oz, A, self.h(4 + self.oz), self.h(6 + self.oz))
        self.send(12, self.at(self.out, self.y, self.oz, A), self.h(10), "z")

    def result(self):
        self.got(3, self.h(3))
        self.got(10, self.h(8))
        self.got(11, self.h(9))
        self.got(12, self.h(10))
        halves = []
        for part, slots in ((A, (4 + self.z, 6 + self.z, 10)), (B, (3, 8, 9))):
            total = self.at(self.part, self.y, self.z, part)[...]
            for k in slots:
                total = total + decoded(self.h(k)[...])
            halves.append(total.reshape(32, 1024))
        return jnp.concatenate(halves, axis=0)


SUM_MESSAGES = 17
GATHER_MESSAGES = 18


def kernel(
    hidden_hbm,
    gate_hbm,
    up_hbm,
    out_hbm,
    head_hbm,
    ff_gain,
    final_gain,
    rescale,
    targets,
    lengths,
    labels,
    scale_grad,
    loss_out,
    x,
    w_in,
    w_out,
    w_out_t,
    w_head,
    w_head_t,
    act,
    tgt,
    part,
    out1,
    out2,
    halves1,
    quarters1,
    halves2,
    quarters2,
    normed,
    grads,
    logits,
    lgrad,
    res,
    stat,
    rows,
    acc,
    local_sem,
    g1_send,
    g1_recv,
    g2_send,
    g2_recv,
    s_send,
    s_recv,
    t_send,
    t_recv,
):
    place = lax.axis_index("mp")
    log = []
    own = pltpu.make_async_copy(hidden_hbm, x.at[place], local_sem.at[0])
    loads = [
        pltpu.make_async_copy(gate_hbm, w_in.at[:, pl.ds(0, 384)], local_sem.at[1]),
        pltpu.make_async_copy(up_hbm, w_in.at[:, pl.ds(384, 384)], local_sem.at[2]),
        pltpu.make_async_copy(out_hbm, w_out, local_sem.at[3]),
        pltpu.make_async_copy(head_hbm, w_head, local_sem.at[4]),
    ]
    own.start()
    for c in loads:
        c.start()

    barrier = pltpu.get_barrier_semaphore()
    for k in range(1, 8):
        pl.semaphore_signal(
            barrier,
            inc=1,
            device_id={"mp": (place + k) % 8},
            device_id_type=pl.DeviceIdType.MESH,
        )
    pl.semaphore_wait(barrier, 7)
    own.wait()

    first = Gather(
        place, lambda y, z, part: x.at[y * 2 + z, pl.ds(*part)], g1_send, g1_recv, log
    )
    first.s0()
    y, z, yp, ym, yo = first.y, first.z, first.yp, first.ym, first.yo

    def target_block(i, _):
        row = targets[pl.ds(i, 1), :].astype(f32)
        tgt[i] = jnp.transpose(jnp.broadcast_to(row, (128, 128)))
        return 0

    def head_block(i, _):
        r = pl.multiple_of((i // 8) * 256, 256)
        c = pl.multiple_of((i % 8) * 256, 256)
        w_head_t[pl.ds(c, 256), pl.ds(r, 256)] = jnp.transpose(
            w_head[pl.ds(r, 256), pl.ds(c, 256)]
        )
        return 0

    def out_block(i, _):
        r = pl.multiple_of((i // 4) * 128, 128)
        c = pl.multiple_of((i % 4) * 256, 256)
        w_out_t[pl.ds(c, 256), pl.ds(r, 128)] = jnp.transpose(
            w_out[pl.ds(r, 128), pl.ds(c, 256)]
        )
        return 0

    lax.fori_loop(0, 8, target_block, 0)
    acc[...] = jnp.zeros_like(acc)
    stat[...] = jnp.zeros_like(stat)
    loads[2].wait()
    lax.fori_loop(0, 12, out_block, 0)
    loads[3].wait()
    first.r1()
    first.r2()
    lax.fori_loop(0, 32, head_block, 0)
    first.r3()

    def feed_forward(e):
        rows2 = x[pl.ds(2 * e, 2)].reshape(256, 1024).astype(f32)
        inverse = lax.rsqrt(jnp.mean(rows2 * rows2, axis=-1, keepdims=True) + epsilon)
        n = (rows2 * inverse * ff_gain[...]).astype(bf16)
        both = jnp.dot(n, w_in[...], preferred_element_type=f32)
        gate, up = both[:, :384], both[:, 384:]
        cube = gate * gate * gate
        activated = gate * (0.5 * (1.0 + jnp.tanh(ROOT * (gate + 0.044715 * cube)))) * up
        act[pl.ds(2 * e, 2)] = activated.reshape(2, 128, 384)
        hidden = (activated * rescale[...]).astype(bf16)
        total = jnp.dot(hidden, w_out[...], preferred_element_type=f32)
        total = total.reshape(2, 2, 4, 16, 1024)
        part[pl.ds(2 * e, 2)] = total
        out1[pl.ds(2 * e, 2)] = coded(total)

    loads[0].wait()
    loads[1].wait()
    first.own()
    feed_forward(y)
    first.r4()
    first.r5()
    first.minus()
    feed_forward(ym)
    first.plus()
    feed_forward(yp)
    first.far()
    feed_forward(yo)

    sums = [
        Sum(place, g, part, out1, halves1, quarters1, s_send.at[g], s_recv.at[g], log)
        for g in range(2)
    ]
    for s in sums:
        s.s0_far()
        s.s0_plus()
        s.s0_minus()
        s.s0_own()
    for s in sums:
        s.s1()
    for s in sums:
        s.s2()
    for s in sums:
        s.s3()

    def gather_of(ref, sends, recvs, g):
        return Gather(
            place,
            lambda y, z, part: ref.at[g * 4 + y, z, pl.ds(*part)],
            sends.at[g],
            recvs.at[g],
            log,
        )

    nexts = [gather_of(normed, g2_send.at[0], g2_recv.at[0], g) for g in range(2)]
    lasts = [gather_of(grads, g2_send.at[1], g2_recv.at[1], g) for g in range(2)]

    def normed_rows(g):
        inputs = x[g * 4 + y, pl.ds(2 * z, 2)].reshape(64, 1024).astype(f32)
        residual = inputs + sums[g].result()
        res[g] = residual
        inverse = lax.rsqrt(jnp.mean(residual * residual, axis=-1, keepdims=True) + epsilon)
        n = (residual * inverse * final_gain[...]).astype(bf16)
        normed[g * 4 + y, z] = n.reshape(4, 16, 1024)

    lane = lax.broadcasted_iota(jnp.int32, (128, 128), 1)

    def logit_block(g, yy):
        b = g * 4 + yy
        n = normed[b].reshape(128, 1024)

        def tile(j, top):
            c = pl.multiple_of(j * TILE, TILE)
            value = jnp.dot(n, w_head[:, pl.ds(c, TILE)], preferred_element_type=f32)
            logits[b, :, pl.ds(c, TILE)] = value
            for k in range(TILE // 128):
                top = jnp.maximum(top, value[:, k * 128 : (k + 1) * 128])
            return top

        top = lax.fori_loop(0, 2048 // TILE, tile, jnp.full((128, 128), -jnp.inf, f32))
        top = jnp.max(top, axis=1, keepdims=True)
        wide = jnp.broadcast_to(top, (128, 128))
        wanted = tgt[b] - (place * 2048).astype(f32) - lane.astype(f32)

        def tally(j, so_far):
            total, hit = so_far
            for k in range(TILE // 128):
                c = pl.multiple_of(j * TILE + k * 128, 128)
                value = logits[b, :, pl.ds(c, 128)]
                total = total + jnp.exp(value - wide)
                hit = hit + jnp.where(wanted == c.astype(f32), value, 0.0)
            return total, hit

        zero = jnp.zeros((128, 128), f32)
        total, hit = lax.fori_loop(0, 2048 // TILE, tally, (zero, zero))
        total = jnp.sum(total, axis=1, keepdims=True)
        hit = jnp.sum(hit, axis=1, keepdims=True)
        table = jnp.where(lane == 0, top, jnp.where(lane == 1, total, hit))
        table = jnp.transpose(table)
        for k in range(3):
            stat[g, place, pl.ds(4 * k + yy, 1), :] = table[k : k + 1]

    def stat_copy(g, k):
        ref = stat.at[g, place]
        return pltpu.make_async_remote_copy(
            src_ref=ref,
            dst_ref=ref,
            send_sem=t_send.at[g, k - 1],
            recv_sem=t_recv.at[g, k - 1],
            device_id={"mp": (place + k) % 8},
            device_id_type=pl.DeviceIdType.MESH,
        )

    def send_stats(g):
        for k in range(1, 8):
            c = stat_copy(g, k)
            c.start()
            log.append(c)

    def wait_stats(g):
        for k in range(1, 8):
            ref = stat.at[g, (place + 8 - k) % 8]
            pltpu.make_async_remote_copy(
                src_ref=ref,
                dst_ref=ref,
                send_sem=t_send.at[g, k - 1],
                recv_sem=t_recv.at[g, k - 1],
                device_id={"mp": (place + k) % 8},
                device_id_type=pl.DeviceIdType.MESH,
            ).wait_recv()

    right = jnp.int32(0)
    whole = jnp.int32(0)
    for e in range(4):
        for c in range(4):
            right = right + jnp.where(labels[e] == c, lengths[e, c], 0)
            whole = whole + lengths[e, c]
    n_right = right.astype(f32)
    n_wrong = (whole - right).astype(f32)

    def loss_rows(g):
        top = stat[g, 0, 0:4]
        for k in range(1, 8):
            top = jnp.maximum(top, stat[g, k, 0:4])
        total = jnp.zeros((4, 128), f32)
        hit = jnp.zeros((4, 128), f32)
        for k in range(8):
            total = total + stat[g, k, 4:8] * jnp.exp(stat[g, k, 0:4] - top)
            hit = hit + stat[g, k, 8:12]
        log_norm = top + jnp.log(total)
        log_probs = hit - log_norm
        row = lax.broadcasted_iota(jnp.int32, (4, 128), 0)
        col = lax.broadcasted_iota(jnp.int32, (4, 128), 1)
        choice = (row % 2) * 2 + col // 64
        length = jnp.zeros((4, 128), jnp.int32)
        label = jnp.zeros((4, 128), jnp.int32)
        for i in range(4):
            e = g * 2 + i // 2
            label = jnp.where(row == i, labels[e], label)
            for s in range(2):
                here = (row == i) & (col // 64 == s)
                length = jnp.where(here, lengths[e, (i % 2) * 2 + s], length)
        valid = col % 64 < length
        correct = choice == label
        counts = length.astype(f32)
        kept = jnp.where(valid, log_probs, 0.0)
        low = jnp.sum(jnp.where(col < 64, kept, 0.0), axis=1, keepdims=True)
        high = jnp.sum(jnp.where(col < 64, 0.0, kept), axis=1, keepdims=True)
        average = jnp.where(col < 64, low, high) / counts
        safe = jnp.where(valid, log_probs, -1.0)
        prob = jnp.exp(safe)
        wrong = valid & ~correct
        likely = jnp.sum(jnp.where(correct, kept, 0.0))
        unlikely = jnp.sum(jnp.where(wrong, jnp.log1p(-prob), 0.0))
        normed_sum = jnp.float32(0.0)
        shares = []
        for i in range(2):
            a = average[2 * i : 2 * i + 2]
            shift = a - jnp.max(jnp.max(a, axis=1, keepdims=True), axis=0, keepdims=True)
            power = jnp.exp(shift)
            bulk = jnp.sum(jnp.sum(power, axis=1, keepdims=True), axis=0, keepdims=True)
            bulk = bulk * (1.0 / 64.0)
            shares.append(power / bulk)
            fine = jnp.where(correct[2 * i : 2 * i + 2], shift - jnp.log(bulk), 0.0)
            normed_sum = normed_sum + jnp.sum(fine) * (1.0 / 64.0)
        share = jnp.concatenate(shares, axis=0)
        weight = jnp.where(correct, -1.0 / n_right, prob / (1.0 - prob) / n_wrong)
        weight = weight - 0.25 * (jnp.where(correct, 1.0, 0.0) - share) / counts
        rows[g, 0:4] = log_norm
        rows[g, 4:8] = jnp.where(valid, weight, 0.0)
        return -likely / n_right - unlikely / n_wrong - 0.25 * normed_sum

    def grad_block(g, yy):
        b = g * 4 + yy
        norm_row = jnp.broadcast_to(rows[g, pl.ds(yy, 1), :], (128, 128))
        weight_row = jnp.broadcast_to(rows[g, pl.ds(4 + yy, 1), :], (128, 128))
        norm = jnp.transpose(norm_row)
        weight = jnp.transpose(weight_row)
        wanted = tgt[b] - (place * 2048).astype(f32) - lane.astype(f32)

        def tile(j, _):
            for k in range(TILE // 128):
                c = pl.multiple_of(j * TILE + k * 128, 128)
                soft = jnp.exp(logits[b, :, pl.ds(c, 128)] - norm)
                hot = jnp.where(wanted == c.astype(f32), 1.0, 0.0)
                lgrad[:, pl.ds(c, 128)] = (weight * (hot - soft)).astype(bf16)
            return 0

        lax.fori_loop(0, 2048 // TILE, tile, 0)

        def side(j, _):
            c = pl.multiple_of(j * TILE, TILE)
            value = jnp.dot(lgrad[...], w_head_t[:, pl.ds(c, TILE)], preferred_element_type=f32)
            value = value.reshape(2, 4, 16, TILE)
            part[b, :, :, :, pl.ds(c, TILE)] = value
            return 0

        lax.fori_loop(0, 1024 // TILE, side, 0)
        out2[b] = coded(part[b])

    normed_rows(0)
    nexts[0].s0()
    normed_rows(1)
    nexts[1].s0()
    nexts[0].r1()
    nexts[0].r2()
    nexts[1].r1()
    nexts[1].r2()
    nexts[0].r3()
    nexts[0].own()
    nexts[0].r4()
    nexts[0].r5()
    logit_block(0, y)
    nexts[1].r3()
    nexts[1].r4()
    nexts[0].minus()
    logit_block(0, ym)
    nexts[1].r5()
    nexts[0].plus()
    logit_block(0, yp)
    nexts[0].far()
    logit_block(0, yo)
    send_stats(0)
    nexts[1].own()
    logit_block(1, y)
    nexts[1].minus()
    logit_block(1, ym)
    wait_stats(0)
    loss = loss_rows(0)

    sums2 = [
        Sum(place, g, part, out2, halves2, quarters2, s_send.at[2 + g], s_recv.at[2 + g], log)
        for g in range(2)
    ]
    grad_block(0, yo)
    sums2[0].s0_far()
    grad_block(0, yp)
    sums2[0].s0_plus()
    grad_block(0, ym)
    sums2[0].s0_minus()
    grad_block(0, y)
    sums2[0].s0_own()
    nexts[1].plus()
    logit_block(1, yp)
    nexts[1].far()
    logit_block(1, yo)
    send_stats(1)
    sums2[0].s1()
    sums2[0].s2()
    wait_stats(1)
    loss = loss + loss_rows(1)
    loss_out[0] = loss
    grad_block(1, yo)
    sums2[1].s0_far()
    sums2[0].s3()
    grad_block(1, yp)
    sums2[1].s0_plus()
    grad_block(1, ym)
    sums2[1].s0_minus()
    grad_block(1, y)
    sums2[1].s0_own()

    def grad_rows(g):
        residual = res[g]
        inverse = lax.rsqrt(jnp.mean(residual * residual, axis=-1, keepdims=True) + epsilon)
        scaled = sums2[g].result() * final_gain[...]
        inner = jnp.mean(scaled * residual, axis=-1, keepdims=True)
        value = inverse * scaled - residual * (inverse * inverse * inverse) * inner
        grads[g * 4 + y, z] = value.astype(bf16).reshape(4, 16, 1024)

    def scale_block(g, yy):
        b = g * 4 + yy
        back = jnp.dot(grads[b].reshape(128, 1024), w_out_t[...], preferred_element_type=f32)
        acc[...] += jnp.sum((back * act[b]).reshape(16, 8, 384), axis=0)

    grad_rows(0)
    lasts[0].s0()
    sums2[1].s1()
    sums2[1].s2()
    lasts[0].r1()
    lasts[0].r2()
    sums2[1].s3()
    lasts[0].r3()
    lasts[0].r4()
    lasts[0].r5()
    grad_rows(1)
    lasts[1].s0()
    lasts[0].own()
    scale_block(0, y)
    lasts[1].r1()
    lasts[1].r2()
    lasts[0].minus()
    scale_block(0, ym)
    lasts[1].r3()
    lasts[0].plus()
    scale_block(0, yp)
    lasts[1].r4()
    lasts[1].r5()
    lasts[0].far()
    scale_block(0, yo)
    lasts[1].own()
    scale_block(1, y)
    lasts[1].minus()
    scale_block(1, ym)
    lasts[1].plus()
    scale_block(1, yp)
    lasts[1].far()
    scale_block(1, yo)
    scale_grad[...] = jnp.sum(acc[...], axis=0, keepdims=True)
    for c in log:
        c.wait_send()


def per_device(
    hidden_in, ff_gain, w_gate, w_up, w_out, ff_rescale, final_gain, w_head, targets, lengths, labels
):
    vmem = pl.BlockSpec(memory_space=pltpu.VMEM)
    smem = pl.BlockSpec(memory_space=pltpu.SMEM)
    hbm = pl.BlockSpec(memory_space=pl.ANY)
    dma = pltpu.SemaphoreType.DMA
    scale_grad, loss = pl.pallas_call(
        kernel,
        out_shape=(
            jax.ShapeDtypeStruct((1, 384), f32),
            jax.ShapeDtypeStruct((1,), f32),
        ),
        in_specs=[hbm] * 5 + [vmem] * 4 + [smem] * 2,
        out_specs=(vmem, smem),
        scratch_shapes=[
            pltpu.VMEM((8, 4, 32, 1024), bf16),
            pltpu.VMEM((1024, 768), bf16),
            pltpu.VMEM((384, 1024), bf16),
            pltpu.VMEM((1024, 384), bf16),
            pltpu.VMEM((1024, 2048), bf16),
            pltpu.VMEM((2048, 1024), bf16),
            pltpu.VMEM((8, 128, 384), f32),
            pltpu.VMEM((8, 128, 128), f32),
            pltpu.VMEM((8, 2, 4, 16, 1024), f32),
            pltpu.VMEM((8, 2, 4, 16, WIDE), jnp.int16),
            pltpu.VMEM((8, 2, 4, 16, WIDE), jnp.int16),
            pltpu.VMEM((2, 11, 2, 16, WIDE), jnp.int16),
            pltpu.VMEM((2, 6, 1, 16, WIDE), jnp.int16),
            pltpu.VMEM((2, 11, 2, 16, WIDE), jnp.int16),
            pltpu.VMEM((2, 6, 1, 16, WIDE), jnp.int16),
            pltpu.VMEM((8, 2, 4, 16, 1024), bf16),
            pltpu.VMEM((8, 2, 4, 16, 1024), bf16),
            pltpu.VMEM((8, 128, 2048), f32),
            pltpu.VMEM((128, 2048), bf16),
            pltpu.VMEM((2, 64, 1024), f32),
            pltpu.VMEM((2, 8, 16, 128), f32),
            pltpu.VMEM((2, 8, 128), f32),
            pltpu.VMEM((8, 384), f32),
            dma((5,)),
            dma((GATHER_MESSAGES,)),
            dma((GATHER_MESSAGES,)),
            dma((2, 2, GATHER_MESSAGES)),
            dma((2, 2, GATHER_MESSAGES)),
            dma((4, SUM_MESSAGES)),
            dma((4, SUM_MESSAGES)),
            dma((2, 7)),
            dma((2, 7)),
        ],
        compiler_params=pltpu.CompilerParams(
            collective_id=0, has_side_effects=True, vmem_limit_bytes=62 * 1024 * 1024
        ),
    )(
        hidden_in.reshape(4, 32, 1024),
        w_gate,
        w_up,
        w_out,
        w_head,
        ff_gain.reshape(1, 1024),
        final_gain.reshape(1, 1024),
        ff_rescale.reshape(1, 384),
        targets.reshape(8, 128),
        lengths,
        labels,
    )
    return (scale_grad.reshape(384), loss)


def solution(mesh):
    return jax.shard_map(
        per_device,
        mesh=mesh,
        in_specs=(
            P(("task", "mp"), None),
            P(),
            P(None, "mp"),
            P(None, "mp"),
            P("mp", None),
            P(("task", "mp")),
            P(),
            P(None, "mp"),
            P("task"),
            P("task", None),
            P("task"),
        ),
        out_specs=(P(("task", "mp")), P("task")),
        check_vma=False,
    )
```

time: 304 us -> 117 us (0.38)
  blocking collectives: 159 us -> 0 us
  Pallas kernels: 0 us -> 112 us
  waiting for transfers between devices: 76.6 us -> 0 us
  matrix products: 23.3 us -> 0 us
  between operations: 19.8 us -> 2.33 us
  other arithmetic: 16.5 us -> 1.28 us
  starting transfers between devices: 4.51 us -> 0 us
    all_to_all x3 -> x0, blocking collectives: 131 us -> none  [the longest x2 97.7 us: summed_on_arrival(): pieces = lax.all_to_all(cut_along(x, dim, count), axis, 0, 0, tiled=True)]
    pallas_call x0 -> x1, Pallas kernels: none -> 112 us  [per_device(): pl.pallas_call(kernel, out_shape=(jax.ShapeDtypeStruct((1, 384), f32), ja...]
    all_gather x1 -> x0, waiting for transfers between devices: 51.8 us -> none  [per_device(): lax.all_gather(resid_grad, 'mp', axis=0, tiled=True)]
    all_gather x1 -> x0, blocking collectives: 28.4 us -> none  [gathered_once(): both, at, found = (lax.all_gather(jnp.concatenate(lines), axis), 0, {})]
    all_to_all x1 -> x0, waiting for transfers between devices: 24.8 us -> none  [sent_to_all(): return lax.all_to_all(copies, axis, split_axis=0, concat_axis=0, tiled=True)]
    dot_general x6 -> x0, matrix products: 23.3 us -> none  [the longest x1 8.79 us: per_device(): lax.dot_general(logit_grad, w_head, contract, preferred_element_type=jnp....]
    reduce_sum x10 -> x0, other arithmetic: 12.8 us -> none  [the longest x2 6.05 us: summed_on_arrival(): return jnp.sum(pieces, axis=0)]
    all_to_all x1 -> x0, starting transfers between devices: 4.47 us -> none  [sent_to_all(): return lax.all_to_all(copies, axis, split_axis=0, concat_axis=0, tiled=True)]
  transfers between devices with their start and end apart: 2 -> 0, of which waited for: 2 -> 0; matrix products, arithmetic and copies ran while one was open for 0% -> 0% of each run, Pallas kernels for 0% -> 0%
where the time goes in v1:
time: 117 us; the launch traced here: 116 us
  Pallas kernels  112 us (96%)
  between operations  2.33 us (2%)
  other arithmetic  1.28 us (1%)
  local copies, waits for them, and re-layouts  1.25 us (1%)
    pallas_call x1, Pallas kernels, per_device(): pl.pallas_call(kernel, out_shape=(jax.ShapeDtypeStruct((1, 384), f32), ja...  112 us

profile of v1, /device:TPU:4, one launch (start us, length us, event | category | flops | bytes accessed | tf_op | source)
XLA Modules:
  0.0 116.5 jit_solution(7054833644216942126)
XLA Ops:
  0.6 1.2 %reshape.25.rescale = f32[1,384]{1,0:T(1,128)} reshape(f32[384]{0:T(512)} %param.16) | data formatting | bytes 3072 | tf_op jit(solution)/shard_map/reshape | solution.py:727
  1.9 111.6 %shard_map.122 = (f32[1,384]{1,0:T(1,128)}, f32[1]{0:T(128)}) custom-call(bf16[4,32,1024]{2,1,0:T(8,128)(2,1)} %bitcast.4, bf16[1024,384]{1,0:T(8,128)(2,1)} %gate_hbm.1, bf16[1024,384]{1,0:T(8,128)(2,1)} %up_hbm.1, bf16[384,1024]{1,0:T(8,128)(2,1)} %out_hbm.1, bf16[1024,2048]{1,0:T(8,128)(2,1)} %head_hbm.1, f32[1,1024]{1,0:T(1,128)} %bitcast.5, ...), custom_call_target="tpu_custom_call" | custom-call | tf_op jit(solution)/shard_map/pallas_call | solution.py:674
  113.5 1.3 %reduce = f32[384]{0:T(512)} reduce(f32[1,384]{1,0:T(1,128)} %get-tuple-element.4, f32[]{:T(128)} %constant.4), dimensions={0}, to_apply=%get-tuple-element.4.reduce_sub_computation | reduce | bytes 3076 | tf_op jit(solution)/shard_map/pallas_call | solution.py:674

commit v2 on v1

--- a/solution.py
+++ b/solution.py
@@ -13,6 +13,7 @@
 epsilon = 1e-06
 ROOT = math.sqrt(2.0 / math.pi)
 TILE = 512
+HALF = 64
 STEPS = 256.0
 TOP = 32700.0
 WIDE = 1024 + 128
@@ -341,7 +342,7 @@
         cube = gate * gate * gate
         activated = gate * (0.5 * (1.0 + jnp.tanh(ROOT * (gate + 0.044715 * cube)))) * up
         act[pl.ds(2 * e, 2)] = activated.reshape(2, 128, 384)
-        hidden = (activated * rescale[...]).astype(bf16)
+        hidden = (activated * rescale[...].reshape(1, 384)).astype(bf16)
         total = jnp.dot(hidden, w_out[...], preferred_element_type=f32)
         total = total.reshape(2, 2, 4, 16, 1024)
         part[pl.ds(2 * e, 2)] = total
@@ -398,35 +399,48 @@
 
     lane = lax.broadcasted_iota(jnp.int32, (128, 128), 1)
 
+    def wanted_of(b):
+        return tgt[b] - (place * 2048).astype(f32) - lane.astype(f32)
+
     def logit_block(g, yy):
         b = g * 4 + yy
         n = normed[b].reshape(128, 1024)
-
-        def tile(j, top):
-            c = pl.multiple_of(j * TILE, TILE)
-            value = jnp.dot(n, w_head[:, pl.ds(c, TILE)], preferred_element_type=f32)
-            logits[b, :, pl.ds(c, TILE)] = value
-            for k in range(TILE // 128):
-                top = jnp.maximum(top, value[:, k * 128 : (k + 1) * 128])
-            return top
-
-        top = lax.fori_loop(0, 2048 // TILE, tile, jnp.full((128, 128), -jnp.inf, f32))
-        top = jnp.max(top, axis=1, keepdims=True)
-        wide = jnp.broadcast_to(top, (128, 128))
-        wanted = tgt[b] - (place * 2048).astype(f32) - lane.astype(f32)
-
-        def tally(j, so_far):
-            total, hit = so_far
-            for k in range(TILE // 128):
-                c = pl.multiple_of(j * TILE + k * 128, 128)
-                value = logits[b, :, pl.ds(c, 128)]
-                total = total + jnp.exp(value - wide)
-                hit = hit + jnp.where(wanted == c.astype(f32), value, 0.0)
-            return total, hit
-
-        zero = jnp.zeros((128, 128), f32)
-        total, hit = lax.fori_loop(0, 2048 // TILE, tally, (zero, zero))
-        total = jnp.sum(total, axis=1, keepdims=True)
+        wanted = wanted_of(b)
+        state = [
+            (
+                jnp.full((HALF, 128), -jnp.inf, f32),
+                jnp.zeros((HALF, 128), f32),
+                jnp.zeros((HALF, 128), f32),
+            )
+            for _ in range(128 // HALF)
+        ]
+
+        def tally(j):
+            for i, (top, total, hit) in enumerate(state):
+                r = slice(i * HALF, (i + 1) * HALF)
+                starts = [j * TILE + k * 128 for k in range(TILE // 128)]
+                values = [logits[b, r, c : c + 128] for c in starts]
+                new = top
+                for value in values:
+                    new = jnp.maximum(new, value)
+                total = total * jnp.exp(top - new)
+                for c, value in zip(starts, values):
+                    total = total + jnp.exp(value - new)
+                    hit = hit + jnp.where(wanted[r] == c, value, 0.0)
+                state[i] = (new, total, hit)
+
+        tiles = 2048 // TILE
+        for j in range(tiles):
+            c = j * TILE
+            logits[b, :, c : c + TILE] = jnp.dot(
+                n, w_head[:, c : c + TILE], preferred_element_type=f32
+            )
+            if j:
+                tally(j - 1)
+        tally(tiles - 1)
+        lanes, total, hit = (jnp.concatenate(v, axis=0) for v in zip(*state))
+        top = jnp.max(lanes, axis=1, keepdims=True)
+        total = jnp.sum(total * jnp.exp(lanes - top), axis=1, keepdims=True)
         hit = jnp.sum(hit, axis=1, keepdims=True)
         table = jnp.where(lane == 0, top, jnp.where(lane == 1, total, hit))
         table = jnp.transpose(table)
@@ -503,9 +517,9 @@
         safe = jnp.where(valid, log_probs, -1.0)
         prob = jnp.exp(safe)
         wrong = valid & ~correct
-        likely = jnp.sum(jnp.where(correct, kept, 0.0))
-        unlikely = jnp.sum(jnp.where(wrong, jnp.log1p(-prob), 0.0))
-        normed_sum = jnp.float32(0.0)
+        terms = jnp.where(correct, kept, 0.0) / n_right
+        terms = terms + jnp.where(wrong, jnp.log1p(-prob), 0.0) / n_wrong
+        fines = []
         shares = []
         for i in range(2):
             a = average[2 * i : 2 * i + 2]
@@ -514,42 +528,49 @@
             bulk = jnp.sum(jnp.sum(power, axis=1, keepdims=True), axis=0, keepdims=True)
             bulk = bulk * (1.0 / 64.0)
             shares.append(power / bulk)
-            fine = jnp.where(correct[2 * i : 2 * i + 2], shift - jnp.log(bulk), 0.0)
-            normed_sum = normed_sum + jnp.sum(fine) * (1.0 / 64.0)
+            fines.append(shift - jnp.log(bulk))
         share = jnp.concatenate(shares, axis=0)
         weight = jnp.where(correct, -1.0 / n_right, prob / (1.0 - prob) / n_wrong)
         weight = weight - 0.25 * (jnp.where(correct, 1.0, 0.0) - share) / counts
         rows[g, 0:4] = log_norm
         rows[g, 4:8] = jnp.where(valid, weight, 0.0)
-        return -likely / n_right - unlikely / n_wrong - 0.25 * normed_sum
-
-    def grad_block(g, yy):
+        fine = jnp.where(correct, jnp.concatenate(fines, axis=0), 0.0)
+        return -terms - fine * (0.25 / 64.0)
+
+    def columns(row):
+        return jnp.transpose(jnp.broadcast_to(row, (128, 128)))
+
+    def softer(g, yy, slot):
         b = g * 4 + yy
-        norm_row = jnp.broadcast_to(rows[g, pl.ds(yy, 1), :], (128, 128))
-        weight_row = jnp.broadcast_to(rows[g, pl.ds(4 + yy, 1), :], (128, 128))
-        norm = jnp.transpose(norm_row)
-        weight = jnp.transpose(weight_row)
-        wanted = tgt[b] - (place * 2048).astype(f32) - lane.astype(f32)
-
-        def tile(j, _):
+        norm = columns(rows[g, pl.ds(yy, 1), :])
+        weight = columns(rows[g, pl.ds(4 + yy, 1), :])
+        wanted = wanted_of(b)
+
+        def step(j):
             for k in range(TILE // 128):
-                c = pl.multiple_of(j * TILE + k * 128, 128)
-                soft = jnp.exp(logits[b, :, pl.ds(c, 128)] - norm)
-                hot = jnp.where(wanted == c.astype(f32), 1.0, 0.0)
-                lgrad[:, pl.ds(c, 128)] = (weight * (hot - soft)).astype(bf16)
-            return 0
-
-        lax.fori_loop(0, 2048 // TILE, tile, 0)
-
-        def side(j, _):
-            c = pl.multiple_of(j * TILE, TILE)
-            value = jnp.dot(lgrad[...], w_head_t[:, pl.ds(c, TILE)], preferred_element_type=f32)
-            value = value.reshape(2, 4, 16, TILE)
-            part[b, :, :, :, pl.ds(c, TILE)] = value
-            return 0
-
-        lax.fori_loop(0, 1024 // TILE, side, 0)
-        out2[b] = coded(part[b])
+                c = j * TILE + k * 128
+                soft = jnp.exp(logits[b, :, c : c + 128] - norm)
+                hot = jnp.where(wanted == c, 1.0, 0.0)
+                lgrad[slot, :, c : c + 128] = (weight * (hot - soft)).astype(bf16)
+
+        return step
+
+    def grad_blocks(g, order, sends):
+        step = softer(g, order[0], 0)
+        for j in range(4):
+            step(j)
+        for i, yy in enumerate(order):
+            b = g * 4 + yy
+            step = softer(g, order[i + 1], (i + 1) % 2) if i + 1 < len(order) else None
+            for j in range(4):
+                value = jnp.dot(
+                    lgrad[i % 2], w_head_t[:, j * 256 : (j + 1) * 256], preferred_element_type=f32
+                )
+                part[b, :, :, :, j * 256 : (j + 1) * 256] = value.reshape(2, 4, 16, 256)
+                if step is not None:
+                    step(j)
+            out2[b] = coded(part[b])
+            sends[i]()
 
     normed_rows(0)
     nexts[0].s0()
@@ -585,14 +606,8 @@
         Sum(place, g, part, out2, halves2, quarters2, s_send.at[2 + g], s_recv.at[2 + g], log)
         for g in range(2)
     ]
-    grad_block(0, yo)
-    sums2[0].s0_far()
-    grad_block(0, yp)
-    sums2[0].s0_plus()
-    grad_block(0, ym)
-    sums2[0].s0_minus()
-    grad_block(0, y)
-    sums2[0].s0_own()
+    s = sums2[0]
+    grad_blocks(0, (yo, yp, ym, y), (s.s0_far, s.s0_plus, s.s0_minus, s.s0_own))
     nexts[1].plus()
     logit_block(1, yp)
     nexts[1].far()
@@ -602,16 +617,9 @@
     sums2[0].s2()
     wait_stats(1)
     loss = loss + loss_rows(1)
-    loss_out[0] = loss
-    grad_block(1, yo)
-    sums2[1].s0_far()
     sums2[0].s3()
-    grad_block(1, yp)
-    sums2[1].s0_plus()
-    grad_block(1, ym)
-    sums2[1].s0_minus()
-    grad_block(1, y)
-    sums2[1].s0_own()
+    s = sums2[1]
+    grad_blocks(1, (yo, yp, ym, y), (s.s0_far, s.s0_plus, s.s0_minus, s.s0_own))
 
     def grad_rows(g):
         residual = res[g]
@@ -628,6 +636,7 @@
 
     grad_rows(0)
     lasts[0].s0()
+    loss_out[0] = jnp.sum(loss)
     sums2[1].s1()
     sums2[1].s2()
     lasts[0].r1()
@@ -659,7 +668,7 @@
     scale_block(1, yp)
     lasts[1].far()
     scale_block(1, yo)
-    scale_grad[...] = jnp.sum(acc[...], axis=0, keepdims=True)
+    scale_grad[...] = jnp.sum(acc[...], axis=0)
     for c in log:
         c.wait_send()
 
@@ -674,7 +683,7 @@
     scale_grad, loss = pl.pallas_call(
         kernel,
         out_shape=(
-            jax.ShapeDtypeStruct((1, 384), f32),
+            jax.ShapeDtypeStruct((384,), f32),
             jax.ShapeDtypeStruct((1,), f32),
         ),
         in_specs=[hbm] * 5 + [vmem] * 4 + [smem] * 2,
@@ -698,7 +707,7 @@
             pltpu.VMEM((8, 2, 4, 16, 1024), bf16),
             pltpu.VMEM((8, 2, 4, 16, 1024), bf16),
             pltpu.VMEM((8, 128, 2048), f32),
-            pltpu.VMEM((128, 2048), bf16),
+            pltpu.VMEM((2, 128, 2048), bf16),
             pltpu.VMEM((2, 64, 1024), f32),
             pltpu.VMEM((2, 8, 16, 128), f32),
             pltpu.VMEM((2, 8, 128), f32),
@@ -724,12 +733,12 @@
         w_head,
         ff_gain.reshape(1, 1024),
         final_gain.reshape(1, 1024),
-        ff_rescale.reshape(1, 384),
+        ff_rescale,
         targets.reshape(8, 128),
         lengths,
         labels,
     )
-    return (scale_grad.reshape(384), loss)
+    return (scale_grad, loss)
 
 
 def solution(mesh):

time: 117 us -> 109 us (0.932)
  Pallas kernels: 112 us -> 105 us
  other arithmetic: 1.28 us -> 0 us
    pallas_call x1, Pallas kernels: 112 us -> 105 us  [per_device(): pl.pallas_call(kernel, out_shape=(jax.ShapeDtypeStruct((384,), f32), jax....]
    pallas_call x1 -> x0, other arithmetic: 1.28 us -> none  [per_device(): pl.pallas_call(kernel, out_shape=(jax.ShapeDtypeStruct((1, 384), f32), ja...]
    unnamed x0 -> x1, local copies, waits for them, and re-layouts: none -> 1.25 us
    reshape x1 -> x0, local copies, waits for them, and re-layouts: 1.25 us -> none  [per_device(): ff_rescale.reshape(1, 384)]
where the time goes in v2:
time: 109 us; the launch traced here: 108 us
  Pallas kernels  105 us (96%)
  between operations  2.41 us (2%)
  local copies, waits for them, and re-layouts  1.25 us (1%)
    pallas_call x1, Pallas kernels, per_device(): pl.pallas_call(kernel, out_shape=(jax.ShapeDtypeStruct((384,), f32), jax....  105 us

profile of v2, /device:TPU:4, one launch (start us, length us, event | category | flops | bytes accessed | tf_op | source)
XLA Modules:
  0.0 108.5 jit_solution(12950428177129944960)
XLA Ops:
  0.6 104.8 %shard_map.122 = (f32[384]{0:T(512)}, f32[1]{0:T(128)}) custom-call(bf16[4,32,1024]{2,1,0:T(8,128)(2,1)} %bitcast.4, bf16[1024,384]{1,0:T(8,128)(2,1)} %gate_hbm.1, bf16[1024,384]{1,0:T(8,128)(2,1)} %up_hbm.1, bf16[384,1024]{1,0:T(8,128)(2,1)} %out_hbm.1, bf16[1024,2048]{1,0:T(8,128)(2,1)} %head_hbm.1, f32[1,1024]{1,0:T(1,128)} %bitcast.5, ...), custom_call_target="tpu_custom_call" | custom-call | tf_op jit(solution)/shard_map/pallas_call | solution.py:683
  105.5 1.2 %copy.15 = f32[384]{0:T(512)} copy(f32[384]{0:T(512)} %get-tuple-element.4) | data formatting | bytes 3072

commit v3 on v2

--- a/solution.py
+++ b/solution.py
@@ -150,12 +150,18 @@
     def q(self, k):
         return self.quarters.at[self.g, k]
 
-    def s0_far(self):
+    def s0_far_y(self):
         yo = self.yo
         for z in range(2):
             self.send(4 + 9 * z, self.at(self.out, yo, z, AP), self.q(0 + z), "p")
             self.send(5 + 9 * z, self.at(self.out, yo, z, AM), self.q(2 + z), "m")
-        self.send(0, self.at(self.out, yo, self.oz, B), self.h(0), "z")
+
+    def s0_far_z(self):
+        self.send(0, self.at(self.out, self.yo, self.oz, B), self.h(0), "z")
+
+    def s0_far(self):
+        self.s0_far_y()
+        self.s0_far_z()
 
     def s0_plus(self):
         self.send(1, self.at(self.out, self.yp, self.oz, B), self.h(1), "z")
@@ -172,11 +178,17 @@
             total = total + decoded(ref[...])
         self.at(self.out, y, z, part)[...] = coded(total)
 
-    def s1(self):
+    def s1b(self):
         self.got(0, self.h(0))
         self.add(self.yo, self.z, B, self.h(0))
         self.send(8, self.at(self.out, self.yo, self.z, BP), self.q(4), "p")
         self.send(9, self.at(self.out, self.yo, self.z, BM), self.q(5), "m")
+
+    def s1(self):
+        self.s1b()
+        self.s1a()
+
+    def s1a(self):
         for z in range(2):
             self.got(4 + 9 * z, self.q(0 + z))
             self.add(self.yp, z, AP, self.q(0 + z))
@@ -230,12 +242,12 @@
     up_hbm,
     out_hbm,
     head_hbm,
-    ff_gain,
-    final_gain,
-    rescale,
-    targets,
-    lengths,
-    labels,
+    ff_gain_hbm,
+    final_gain_hbm,
+    rescale_hbm,
+    targets_hbm,
+    lengths_hbm,
+    labels_hbm,
     scale_grad,
     loss_out,
     x,
@@ -261,6 +273,12 @@
     stat,
     rows,
     acc,
+    ff_gain,
+    final_gain,
+    rescale,
+    targets,
+    lengths,
+    labels,
     local_sem,
     g1_send,
     g1_recv,
@@ -280,8 +298,21 @@
         pltpu.make_async_copy(out_hbm, w_out, local_sem.at[3]),
         pltpu.make_async_copy(head_hbm, w_head, local_sem.at[4]),
     ]
+    small = [
+        pltpu.make_async_copy(src, dst, local_sem.at[5 + k])
+        for k, (src, dst) in enumerate(
+            (
+                (targets_hbm, targets),
+                (ff_gain_hbm, ff_gain),
+                (rescale_hbm, rescale),
+                (final_gain_hbm, final_gain),
+                (lengths_hbm, lengths),
+                (labels_hbm, labels),
+            )
+        )
+    ]
     own.start()
-    for c in loads:
+    for c in (*small, *loads):
         c.start()
 
     barrier = pltpu.get_barrier_semaphore()
@@ -322,6 +353,8 @@
         )
         return 0
 
+    for c in small:
+        c.wait()
     lax.fori_loop(0, 8, target_block, 0)
     acc[...] = jnp.zeros_like(acc)
     stat[...] = jnp.zeros_like(stat)
@@ -367,8 +400,10 @@
     ]
     for s in sums:
         s.s0_far()
+    for s in sums:
         s.s0_plus()
         s.s0_minus()
+    for s in sums:
         s.s0_own()
     for s in sums:
         s.s1()
@@ -599,6 +634,11 @@
     logit_block(1, y)
     nexts[1].minus()
     logit_block(1, ym)
+    nexts[1].plus()
+    logit_block(1, yp)
+    nexts[1].far()
+    logit_block(1, yo)
+    send_stats(1)
     wait_stats(0)
     loss = loss_rows(0)
 
@@ -608,11 +648,6 @@
     ]
     s = sums2[0]
     grad_blocks(0, (yo, yp, ym, y), (s.s0_far, s.s0_plus, s.s0_minus, s.s0_own))
-    nexts[1].plus()
-    logit_block(1, yp)
-    nexts[1].far()
-    logit_block(1, yo)
-    send_stats(1)
     sums2[0].s1()
     sums2[0].s2()
     wait_stats(1)
@@ -634,6 +669,7 @@
         back = jnp.dot(grads[b].reshape(128, 1024), w_out_t[...], preferred_element_type=f32)
         acc[...] += jnp.sum((back * act[b]).reshape(16, 8, 384), axis=0)
 
+    sent = len(log)
     grad_rows(0)
     lasts[0].s0()
     loss_out[0] = jnp.sum(loss)
@@ -647,6 +683,8 @@
     lasts[0].r5()
     grad_rows(1)
     lasts[1].s0()
+    for c in log[:sent]:
+        c.wait_send()
     lasts[0].own()
     scale_block(0, y)
     lasts[1].r1()
@@ -669,7 +707,7 @@
     lasts[1].far()
     scale_block(1, yo)
     scale_grad[...] = jnp.sum(acc[...], axis=0)
-    for c in log:
+    for c in log[sent:]:
         c.wait_send()
 
 
@@ -686,7 +724,7 @@
             jax.ShapeDtypeStruct((384,), f32),
             jax.ShapeDtypeStruct((1,), f32),
         ),
-        in_specs=[hbm] * 5 + [vmem] * 4 + [smem] * 2,
+        in_specs=[hbm] * 11,
         out_specs=(vmem, smem),
         scratch_shapes=[
             pltpu.VMEM((8, 4, 32, 1024), bf16),
@@ -712,7 +750,13 @@
             pltpu.VMEM((2, 8, 16, 128), f32),
             pltpu.VMEM((2, 8, 128), f32),
             pltpu.VMEM((8, 384), f32),
-            dma((5,)),
+            pltpu.VMEM((1, 1024), f32),
+            pltpu.VMEM((1, 1024), f32),
+            pltpu.VMEM((384,), f32),
+            pltpu.VMEM((8, 128), jnp.int32),
+            pltpu.SMEM((4, 4), jnp.int32),
+            pltpu.SMEM((4,), jnp.int32),
+            dma((11,)),
             dma((GATHER_MESSAGES,)),
             dma((GATHER_MESSAGES,)),
             dma((2, 2, GATHER_MESSAGES)),

time: 109 us -> 105 us (0.963)
  Pallas kernels: 105 us -> 101 us
    pallas_call x1, Pallas kernels: 105 us -> 101 us  [per_device(): pl.pallas_call(kernel, out_shape=(jax.ShapeDtypeStruct((384,), f32), jax....]
where the time goes in v3:
time: 105 us
  Pallas kernels  101 us (96%)
  between operations  2.41 us (2%)
  local copies, waits for them, and re-layouts  1.25 us (1%)
    pallas_call x1, Pallas kernels, per_device(): pl.pallas_call(kernel, out_shape=(jax.ShapeDtypeStruct((384,), f32), jax....  101 us

profile of v3, /device:TPU:4, one launch (start us, length us, event | category | flops | bytes accessed | tf_op | source)
XLA Modules:
  0.0 104.9 jit_solution(1660127639201724140)
XLA Ops:
  0.6 101.3 %shard_map.122 = (f32[384]{0:T(512)}, f32[1]{0:T(128)}) custom-call(bf16[4,32,1024]{2,1,0:T(8,128)(2,1)} %bitcast.4, bf16[1024,384]{1,0:T(8,128)(2,1)} %gate_hbm.1, bf16[1024,384]{1,0:T(8,128)(2,1)} %up_hbm.1, bf16[384,1024]{1,0:T(8,128)(2,1)} %out_hbm.1, bf16[1024,2048]{1,0:T(8,128)(2,1)} %head_hbm.1, f32[1,1024]{1,0:T(1,128)} %bitcast.5, ...), custom_call_target="tpu_custom_call" | custom-call | tf_op jit(solution)/shard_map/pallas_call | solution.py:721
  101.9 1.2 %copy.15 = f32[384]{0:T(512)} copy(f32[384]{0:T(512)} %get-tuple-element.4) | data formatting | bytes 3072

commit v4 on v3

--- a/solution.py
+++ b/solution.py
@@ -128,8 +128,14 @@
         self.have(15, self.ym, self.oz, B)
 
     def far(self):
+        self.far_near()
+        self.far_across()
+
+    def far_near(self):
         self.have(10, self.yo, self.z, AP)
         self.have(11, self.yo, self.z, AM)
+
+    def far_across(self):
         self.have(12, self.yo, self.oz, AP)
         self.have(13, self.yo, self.oz, AM)
         self.have(16, self.yo, self.oz, BP)
@@ -366,33 +372,36 @@
     lax.fori_loop(0, 32, head_block, 0)
     first.r3()
 
-    def feed_forward(e):
-        rows2 = x[pl.ds(2 * e, 2)].reshape(256, 1024).astype(f32)
+    def feed_forward(first_chunk, count):
+        here = pl.ds(first_chunk, count)
+        rows2 = x[here].reshape(count * 128, 1024).astype(f32)
         inverse = lax.rsqrt(jnp.mean(rows2 * rows2, axis=-1, keepdims=True) + epsilon)
         n = (rows2 * inverse * ff_gain[...]).astype(bf16)
         both = jnp.dot(n, w_in[...], preferred_element_type=f32)
         gate, up = both[:, :384], both[:, 384:]
         cube = gate * gate * gate
         activated = gate * (0.5 * (1.0 + jnp.tanh(ROOT * (gate + 0.044715 * cube)))) * up
-        act[pl.ds(2 * e, 2)] = activated.reshape(2, 128, 384)
+        act[here] = activated.reshape(count, 128, 384)
         hidden = (activated * rescale[...].reshape(1, 384)).astype(bf16)
         total = jnp.dot(hidden, w_out[...], preferred_element_type=f32)
-        total = total.reshape(2, 2, 4, 16, 1024)
-        part[pl.ds(2 * e, 2)] = total
-        out1[pl.ds(2 * e, 2)] = coded(total)
+        total = total.reshape(count, 2, 4, 16, 1024)
+        part[here] = total
+        out1[here] = coded(total)
 
     loads[0].wait()
     loads[1].wait()
     first.own()
-    feed_forward(y)
+    feed_forward(2 * y, 2)
     first.r4()
     first.r5()
     first.minus()
-    feed_forward(ym)
+    feed_forward(2 * ym, 2)
     first.plus()
-    feed_forward(yp)
-    first.far()
-    feed_forward(yo)
+    feed_forward(2 * yp, 2)
+    first.far_near()
+    feed_forward(2 * yo + z, 1)
+    first.far_across()
+    feed_forward(2 * yo + 1 - z, 1)
 
     sums = [
         Sum(place, g, part, out1, halves1, quarters1, s_send.at[g], s_recv.at[g], log)

time: 105 us -> 104 us (level)
    pallas_call x1, Pallas kernels: 101 us -> 100 us  [per_device(): pl.pallas_call(kernel, out_shape=(jax.ShapeDtypeStruct((384,), f32), jax....]
where the time goes in v4:
time: 104 us
  Pallas kernels  100 us (96%)
  between operations  2.41 us (2%)
  local copies, waits for them, and re-layouts  1.25 us (1%)
    pallas_call x1, Pallas kernels, per_device(): pl.pallas_call(kernel, out_shape=(jax.ShapeDtypeStruct((384,), f32), jax....  100 us

profile of v4, /device:TPU:4, one launch (start us, length us, event | category | flops | bytes accessed | tf_op | source)
XLA Modules:
  0.0 103.9 jit_solution(1649915044689118009)
XLA Ops:
  0.6 100.2 %shard_map.122 = (f32[384]{0:T(512)}, f32[1]{0:T(128)}) custom-call(bf16[4,32,1024]{2,1,0:T(8,128)(2,1)} %bitcast.4, bf16[1024,384]{1,0:T(8,128)(2,1)} %gate_hbm.1, bf16[1024,384]{1,0:T(8,128)(2,1)} %up_hbm.1, bf16[384,1024]{1,0:T(8,128)(2,1)} %out_hbm.1, bf16[1024,2048]{1,0:T(8,128)(2,1)} %head_hbm.1, f32[1,1024]{1,0:T(1,128)} %bitcast.5, ...), custom_call_target="tpu_custom_call" | custom-call | tf_op jit(solution)/shard_map/pallas_call | solution.py:730
  100.9 1.2 %copy.15 = f32[384]{0:T(512)} copy(f32[384]{0:T(512)} %get-tuple-element.4) | data formatting | bytes 3072
